TPU v7x, 32 devices: a whole 2x2x4 slice. The times are simulated.
32 devices in a mesh: gx: 2 (over y), gy: 4 (over x, core), gz: 4 (over z).
Axes of the slice: x: 2, y: 2, z: 4, core: 2. Of those that a mesh axis runs over, the one named last changes fastest.
Arguments:
- volume: float32 [16, 64, 512], P(('gx', 'gy'), None, 'gz'), may hold values from 0 to 1
- levels: int32 [4], replicated, may hold values from 0 to 255
Outputs:
- labelling: float32 [4, 16, 64, 512], P(None, 'gx', 'gy', 'gz')
- centers: float32 [4], replicated
All inputs are finite; a program needn't handle non-finite values.
Results may differ from a plain program's by a relative error of at most 0.0001.
Values sent between devices are 32-bit elements; how exact they have to be, the bound alone decides.
A program may use at most 64 MiB of HBM per device.

v0:
```python
import jax
import jax.numpy as jnp
from jax import lax
from jax.sharding import PartitionSpec as P

ITERS = 2


tau_step = 0.25
sigma_step = 0.25
smooth_weight = 0.5
prior_weight = 1.0


def with_halo(block, sides, width):
    for axis, dim in sides:
        count = lax.axis_size(axis)
        forward = [(i, i + 1) for i in range(count - 1)]
        backward = [(target, source) for source, target in forward]
        low = lax.ppermute(
            lax.slice_in_dim(block, block.shape[dim] - width, None, axis=dim), axis, forward
        )
        high = lax.ppermute(lax.slice_in_dim(block, 0, width, axis=dim), axis, backward)
        block = jnp.concatenate([low, block, high], axis=dim)
    return block


def project_simplex(values):
    how_many = values.shape[0]
    threshold = None
    for subset in range(1, 1 << how_many):
        members = [label_index for label_index in range(how_many) if subset >> label_index & 1]
        summed = values[members[0]]
        for label_index in members[1:]:
            summed = summed + values[label_index]
        candidate = (summed - 1.0) / float(len(members))
        threshold = candidate if threshold is None else jnp.maximum(threshold, candidate)
    return jnp.maximum(values - threshold[None], 0.0)


def bounds(start, total, extent):
    position = start - 1 + jnp.arange(extent + 1, dtype=jnp.int32)
    return (position >= 0, position < total - 1)


def local(volume, levels):
    thickness = volume.shape[0]
    x_start = (lax.axis_index("gx") * lax.axis_size("gy") + lax.axis_index("gy")) * thickness
    x_total = thickness * lax.axis_size("gx") * lax.axis_size("gy")
    y_start = 0
    y_total = volume.shape[1]
    z_start = lax.axis_index("gz") * volume.shape[2]
    z_total = volume.shape[2] * lax.axis_size("gz")
    extent = volume.shape
    how_many = levels.shape[0]
    inside_x, ahead_x = bounds(x_start, x_total, extent[0])
    inside_y, ahead_y = bounds(y_start, y_total, extent[1])
    inside_z, ahead_z = bounds(z_start, z_total, extent[2])
    inside = (inside_x[:, None, None] & inside_y[None, :, None] & inside_z[None, None, :]).astype(
        jnp.float32
    )
    base_levels = levels.astype(jnp.float32) / 255.0
    centers = base_levels
    starting = (volume[None] - base_levels[:, None, None, None]) ** 2
    labelling = project_simplex(1.0 / how_many - tau_step * starting)
    smoothed = labelling
    dual_field = jnp.zeros((how_many, 3, extent[0] + 1, extent[1] + 1, extent[2] + 1), jnp.float32)
    for iteration in range(ITERS):
        padded = with_halo(smoothed, ((("gx", "gy"), 1), ("gz", 3)), 1)
        padded = jnp.pad(padded, ((0, 0), (0, 0), (1, 1), (0, 0)))
        corner = padded[:, :-1, :-1, :-1]
        grad_x = jnp.where(ahead_x[:, None, None], padded[:, 1:, :-1, :-1] - corner, 0.0)
        grad_y = jnp.where(ahead_y[None, :, None], padded[:, :-1, 1:, :-1] - corner, 0.0)
        grad_z = jnp.where(ahead_z[None, None, :], padded[:, :-1, :-1, 1:] - corner, 0.0)
        stepped = dual_field + sigma_step * jnp.stack([grad_x, grad_y, grad_z], axis=1)
        length = jnp.sqrt(
            stepped[:, 0] * stepped[:, 0]
            + stepped[:, 1] * stepped[:, 1]
            + stepped[:, 2] * stepped[:, 2]
        )
        shrink = inside / jnp.maximum(1.0, length / smooth_weight)
        dual_field = stepped * shrink[:, None]
        divergence = (
            dual_field[:, 0, 1:, 1:, 1:]
            - dual_field[:, 0, :-1, 1:, 1:]
            + (dual_field[:, 1, 1:, 1:, 1:] - dual_field[:, 1, 1:, :-1, 1:])
            + (dual_field[:, 2, 1:, 1:, 1:] - dual_field[:, 2, 1:, 1:, :-1])
        )
        fidelity = (volume[None] - centers[:, None, None, None]) ** 2
        updated = project_simplex(labelling + tau_step * (divergence - fidelity))
        smoothed = 2.0 * updated - labelling
        labelling = updated
        sizes_local = jnp.sum(labelling, axis=(1, 2, 3))
        weighted = jnp.sum(labelling * volume[None], axis=(1, 2, 3))
        sizes_all, weighted_all = lax.psum((sizes_local, weighted), ("gx", "gy", "gz"))
        centers = (weighted_all + prior_weight * base_levels) / (sizes_all + prior_weight)
    labelling = lax.all_to_all(labelling, "gy", split_axis=2, concat_axis=1, tiled=True)
    return (labelling, centers)


def solution(mesh):
    return jax.shard_map(
        local,
        mesh=mesh,
        in_specs=(P(("gx", "gy"), None, "gz"), P()),
        out_specs=(P(None, "gx", "gy", "gz"), P()),
        check_vma=False,
    )
```

profile of v0, /device:TPU:0, one launch (start us, length us, event | category | flops | bytes accessed | tf_op | source)
XLA Modules:
  0.0 159.2 jit_solution(3588290688517704985)
XLA Ops:
  0.6 0.7 convert_multiply_fusion
  1.3 0.9 multiply_subtract_fusion.1
  2.2 0.1 maximum_bitcast_fusion.2
  2.4 0.6 copy-done.8
  3.0 1.0 subtract_maximum_fusion.2
  4.0 2.4 %collective-permute-start = (f32[4,1,64,128]{3,2,1,0:T(8,128)S(1)}, f32[4,1,64,128]{3,2,1,0:T(8,128)S(1)}, u32[]{:S(2)}, u32[]{:S(2)}) collective-permute-start(f32[4,1,64,128]{3,2,1,0:T(8,128)S(1)} %get-tuple-element.24), channel_id=1, source_target_pairs={{0,4},{4,8},{8,12},{12,16},{16,20},{20,24},{24,28},{1,5},{5,9},{9,... | collective-permute-start | bytes 393224 | tf_op jit(solution)/shard_map/ppermute | solution.py:20
  6.4 1.3 collective-permute-start.1
  8.0 3.7 %collective-permute-done.1 = f32[4,1,64,128]{3,2,1,0:T(8,128)S(1)} collective-permute-done((f32[4,1,64,128]{3,2,1,0:T(8,128)S(1)}, f32[4,1,64,128]{3,2,1,0:T(8,128)S(1)}, u32[]{:S(2)}, u32[]{:S(2)}) %collective-permute-start.1) | collective-permute-done | bytes 131104 | tf_op jit(solution)/shard_map/ppermute | solution.py:23
  11.8 0.2 fusion.66
  12.0 3.5 %collective-permute-start.2 = (f32[4,4,64,1]{3,2,1,0:T(8,128)S(1)}, f32[4,4,64,1]{3,2,1,0:T(8,128)S(1)}, u32[]{:S(2)}, u32[]{:S(2)}) collective-permute-start(f32[4,4,64,1]{3,2,1,0:T(8,128)S(1)} %get-tuple-element.19), channel_id=1, source_target_pairs={{0,1},{1,2},{2,3},{4,5},{5,6},{6,7},{8,9},{9,10},{10,11},{12,13},{... | collective-permute-start | bytes 12296 | tf_op jit(solution)/shard_map/ppermute | solution.py:20
  15.5 1.3 collective-permute-start.3
  16.8 8.4 %collective-permute-done.2 = f32[4,4,64,1]{3,2,1,0:T(8,128)S(1)} collective-permute-done((f32[4,4,64,1]{3,2,1,0:T(8,128)S(1)}, f32[4,4,64,1]{3,2,1,0:T(8,128)S(1)}, u32[]{:S(2)}, u32[]{:S(2)}) %collective-permute-start.2) | collective-permute-done | bytes 4128 | tf_op jit(solution)/shard_map/ppermute | solution.py:20
  25.2 4.7 %collective-permute-done.3 = f32[4,4,64,1]{3,2,1,0:T(8,128)S(1)} collective-permute-done((f32[4,4,64,1]{3,2,1,0:T(8,128)S(1)}, f32[4,4,64,1]{3,2,1,0:T(8,128)S(1)}, u32[]{:S(2)}, u32[]{:S(2)}) %collective-permute-start.3) | collective-permute-done | bytes 4128 | tf_op jit(solution)/shard_map/ppermute | solution.py:23
  29.9 0.5 select_maximum_fusion.4
  30.4 0.5 fusion.29
  30.9 0.2 fusion.2
  31.2 0.5 fusion.30
  31.7 0.3 fusion.1
  32.0 0.5 copy-done.4
  32.6 0.5 fusion.41
  33.0 0.1 maximum_bitcast_fusion.1
  33.1 0.9 copy-done
  34.1 1.1 multiply_reduce_fusion.1
  35.2 0.7 copy-done.2
  35.9 0.7 fusion.67
  36.6 4.7 %collective-permute-start.4 = (f32[4,1,64,128]{3,2,1,0:T(8,128)}, f32[4,1,64,128]{3,2,1,0:T(8,128)}, u32[]{:S(2)}, u32[]{:S(2)}) collective-permute-start(f32[4,1,64,128]{3,2,1,0:T(8,128)} %get-tuple-element.22), channel_id=1, source_target_pairs={{0,4},{4,8},{8,12},{12,16},{16,20},{20,24},{24,28},{1,5},{5,9},{9,... | collective-permute-start | bytes 393224 | tf_op jit(solution)/shard_map/ppermute | solution.py:20
  41.3 1.3 collective-permute-start.5
  42.6 44.4 %all-reduce.3 = (f32[4]{0:T(128)}, f32[4]{0:T(128)}) all-reduce(f32[4]{0:T(128)} %get-tuple-element.3, f32[4]{0:T(128)} %get-tuple-element.2), channel_id=1, replica_groups=mesh['gx'=2,'gy'=4,'gz'=4] {'gx','gy','gz'}, use_global_device_ids=true, to_apply=%region_3.4 | all-reduce | flops 8 | bytes 64 | tf_op jit(solution)/shard_map/psum | solution.py:95
  87.0 1.1 pad_maximum_fusion.2
  88.2 0.2 fusion.65
  88.4 2.3 %collective-permute-start.6 = (f32[4,4,64,1]{3,2,1,0:T(8,128)S(1)}, f32[4,4,64,1]{3,2,1,0:T(8,128)S(1)}, u32[]{:S(2)}, u32[]{:S(2)}) collective-permute-start(f32[4,4,64,1]{3,2,1,0:T(8,128)S(1)} %get-tuple-element.17), channel_id=1, source_target_pairs={{0,1},{1,2},{2,3},{4,5},{5,6},{6,7},{8,9},{9,10},{10,11},{12,13},{... | collective-permute-start | bytes 12296 | tf_op jit(solution)/shard_map/ppermute | solution.py:20
  90.7 1.3 collective-permute-start.7
  92.1 9.2 %collective-permute-done.6 = f32[4,4,64,1]{3,2,1,0:T(8,128)S(1)} collective-permute-done((f32[4,4,64,1]{3,2,1,0:T(8,128)S(1)}, f32[4,4,64,1]{3,2,1,0:T(8,128)S(1)}, u32[]{:S(2)}, u32[]{:S(2)}) %collective-permute-start.6) | collective-permute-done | bytes 4128 | tf_op jit(solution)/shard_map/ppermute | solution.py:20
  101.3 4.1 %collective-permute-done.7 = f32[4,4,64,1]{3,2,1,0:T(8,128)S(1)} collective-permute-done((f32[4,4,64,1]{3,2,1,0:T(8,128)S(1)}, f32[4,4,64,1]{3,2,1,0:T(8,128)S(1)}, u32[]{:S(2)}, u32[]{:S(2)}) %collective-permute-start.7) | collective-permute-done | bytes 4128 | tf_op jit(solution)/shard_map/ppermute | solution.py:23
  105.5 1.5 select_maximum_fusion
  107.0 0.4 fusion.16
  107.4 0.4 fusion
  107.9 0.5 copy-done.7
  108.3 0.5 fusion.9
  108.9 0.5 broadcast_multiply_fusion
  109.4 1.2 copy-done.1
  110.6 0.8 fusion.35
  111.5 0.2 multiply_reduce_fusion
  111.6 0.9 copy.8
  112.5 3.9 %all-to-all-start = ((f32[4,2,64,128]{3,1,0,2:T(2,128)}), f32[4,2,64,128]{3,1,0,2:T(2,128)S(1)}, u32[]{:S(2)}, u32[]{:S(2)}) async-start(f32[4,2,64,128]{3,1,0,2:T(2,128)} %copy.8), calls=%async_computation | async-start | bytes 524288 | tf_op jit(solution)/shard_map/all_to_all | solution.py:97
  116.4 41.5 %all-reduce.2 = (f32[4]{0:T(128)S(1)}, f32[4]{0:T(128)S(1)}) all-reduce(f32[4]{0:T(128)S(1)} %get-tuple-element.5, f32[4]{0:T(128)S(1)} %get-tuple-element.4), channel_id=1, replica_groups=mesh['gx'=2,'gy'=4,'gz'=4] {'gx','gy','gz'}, use_global_device_ids=true, to_apply=%region_7.8 | all-reduce | flops 8 | bytes 64 | tf_op jit(solution)/shard_map/psum | solution.py:95
  157.9 0.5 add_divide_fusion
  158.5 0.7 copy.10
  (47 shorter events, 0.6 us)
Async XLA Ops:
  2.4 0.6 copy-start.8
  4.0 4.0 %collective-permute-start = (f32[4,1,64,128]{3,2,1,0:T(8,128)S(1)}, f32[4,1,64,128]{3,2,1,0:T(8,128)S(1)}, u32[]{:S(2)}, u32[]{:S(2)}) collective-permute-start(f32[4,1,64,128]{3,2,1,0:T(8,128)S(1)} %get-tuple-element.24), channel_id=1, source_target_pairs={{0,4},{4,8},{8,12},{12,16},{16,20},{20,24},{24,28},{1,5},{5,9},{9,... | collective-permute-start | bytes 393224 | tf_op jit(solution)/shard_map/ppermute | solution.py:20
  6.4 5.3 %collective-permute-start.1 = (f32[4,1,64,128]{3,2,1,0:T(8,128)S(1)}, f32[4,1,64,128]{3,2,1,0:T(8,128)S(1)}, u32[]{:S(2)}, u32[]{:S(2)}) collective-permute-start(f32[4,1,64,128]{3,2,1,0:T(8,128)S(1)} %get-tuple-element.25), channel_id=1, source_target_pairs={{4,0},{8,4},{12,8},{16,12},{20,16},{24,20},{28,24},{5,1},{9,5},{13... | collective-permute-start | bytes 393224 | tf_op jit(solution)/shard_map/ppermute | solution.py:23
  7.9 23.2 %copy-start.6 = (f32[3,65,129]{2,1,0:T(8,128)}, f32[3,65,129]{2,1,0:T(8,128)S(1)}, u32[]{:S(2)}) copy-start(f32[3,65,129]{2,1,0:T(8,128)S(1)} %and_convert_fusion) | copy-start | bytes 301864
  12.0 13.2 %collective-permute-start.2 = (f32[4,4,64,1]{3,2,1,0:T(8,128)S(1)}, f32[4,4,64,1]{3,2,1,0:T(8,128)S(1)}, u32[]{:S(2)}, u32[]{:S(2)}) collective-permute-start(f32[4,4,64,1]{3,2,1,0:T(8,128)S(1)} %get-tuple-element.19), channel_id=1, source_target_pairs={{0,1},{1,2},{2,3},{4,5},{5,6},{6,7},{8,9},{9,10},{10,11},{12,13},{... | collective-permute-start | bytes 12296 | tf_op jit(solution)/shard_map/ppermute | solution.py:20
  15.5 14.4 %collective-permute-start.3 = (f32[4,4,64,1]{3,2,1,0:T(8,128)S(1)}, f32[4,4,64,1]{3,2,1,0:T(8,128)S(1)}, u32[]{:S(2)}, u32[]{:S(2)}) collective-permute-start(f32[4,4,64,1]{3,2,1,0:T(8,128)S(1)} %get-tuple-element.20), channel_id=1, source_target_pairs={{1,0},{2,1},{3,2},{5,4},{6,5},{7,6},{9,8},{10,9},{11,10},{13,12},{... | collective-permute-start | bytes 12296 | tf_op jit(solution)/shard_map/ppermute | solution.py:23
  16.8 14.1 %copy-start.14 = (pred[65]{0:T(512)(128)(4,1)}, pred[65]{0:T(512)(128)(4,1)S(1)}, u32[]{:S(2)}) copy-start(pred[65]{0:T(512)(128)(4,1)S(1)} %fusion.62) | copy-start | bytes 199
  31.7 0.8 copy-start.4
  31.7 0.9 copy-start.9
  32.5 1.5 copy-start
  34.1 2.6 %copy-start.11 = (f32[2,64,128]{2,1,0:T(8,128)}, f32[2,64,128]{2,1,0:T(8,128)S(1)}, u32[]{:S(2)}) copy-start(f32[2,64,128]{2,1,0:T(8,128)S(1)} %maximum_bitcast_fusion.1) | copy-start | bytes 196612
  34.1 58.0 %copy-start.13 = (s32[4]{0:T(128)S(1)}, s32[4]{0:T(128)}, u32[]{:S(2)}) copy-start(s32[4]{0:T(128)} %param.3) | copy-start | bytes 52
  35.2 0.7 copy-start.2
  36.6 50.4 %collective-permute-start.4 = (f32[4,1,64,128]{3,2,1,0:T(8,128)}, f32[4,1,64,128]{3,2,1,0:T(8,128)}, u32[]{:S(2)}, u32[]{:S(2)}) collective-permute-start(f32[4,1,64,128]{3,2,1,0:T(8,128)} %get-tuple-element.22), channel_id=1, source_target_pairs={{0,4},{4,8},{8,12},{12,16},{16,20},{20,24},{24,28},{1,5},{5,9},{9,... | collective-permute-start | bytes 393224 | tf_op jit(solution)/shard_map/ppermute | solution.py:20
  41.3 45.7 %collective-permute-start.5 = (f32[4,1,64,128]{3,2,1,0:T(8,128)}, f32[4,1,64,128]{3,2,1,0:T(8,128)}, u32[]{:S(2)}, u32[]{:S(2)}) collective-permute-start(f32[4,1,64,128]{3,2,1,0:T(8,128)} %get-tuple-element.23), channel_id=1, source_target_pairs={{4,0},{8,4},{12,8},{16,12},{20,16},{24,20},{28,24},{5,1},{9,5},{13... | collective-permute-start | bytes 393224 | tf_op jit(solution)/shard_map/ppermute | solution.py:23
  87.0 5.0 %copy-start.16 = (f32[4]{0:T(128)S(1)}, f32[4]{0:T(128)}, u32[]{:S(2)}) copy-start(f32[4]{0:T(128)} %get-tuple-element.8) | copy-start | bytes 52
  87.0 5.0 %copy-start.17 = (f32[4]{0:T(128)S(1)}, f32[4]{0:T(128)}, u32[]{:S(2)}) copy-start(f32[4]{0:T(128)} %get-tuple-element.9) | copy-start | bytes 52
  87.0 18.4 %copy-start.3 = (f32[4,2,64,128]{3,2,1,0:T(8,128)S(1)}, f32[4,2,64,128]{3,2,1,0:T(8,128)}, u32[]{:S(2)}) copy-start(f32[4,2,64,128]{3,2,1,0:T(8,128)} %copy-done.2) | copy-start | bytes 786436
  88.2 18.8 %copy-start.15 = (pred[65]{0:T(512)(128)(4,1)S(1)}, pred[65]{0:T(512)(128)(4,1)}, u32[]{:S(2)}) copy-start(pred[65]{0:T(512)(128)(4,1)} %copy-done.14) | copy-start | bytes 199
  88.4 12.9 %collective-permute-start.6 = (f32[4,4,64,1]{3,2,1,0:T(8,128)S(1)}, f32[4,4,64,1]{3,2,1,0:T(8,128)S(1)}, u32[]{:S(2)}, u32[]{:S(2)}) collective-permute-start(f32[4,4,64,1]{3,2,1,0:T(8,128)S(1)} %get-tuple-element.17), channel_id=1, source_target_pairs={{0,1},{1,2},{2,3},{4,5},{5,6},{6,7},{8,9},{9,10},{10,11},{12,13},{... | collective-permute-start | bytes 12296 | tf_op jit(solution)/shard_map/ppermute | solution.py:20
  90.7 14.7 %collective-permute-start.7 = (f32[4,4,64,1]{3,2,1,0:T(8,128)S(1)}, f32[4,4,64,1]{3,2,1,0:T(8,128)S(1)}, u32[]{:S(2)}, u32[]{:S(2)}) collective-permute-start(f32[4,4,64,1]{3,2,1,0:T(8,128)S(1)} %get-tuple-element.18), channel_id=1, source_target_pairs={{1,0},{2,1},{3,2},{5,4},{6,5},{7,6},{9,8},{10,9},{11,10},{13,12},{... | collective-permute-start | bytes 12296 | tf_op jit(solution)/shard_map/ppermute | solution.py:23
  107.4 0.9 copy-start.7
  108.8 1.8 %copy-start.1 = (f32[4,3,3,65,129]{4,3,2,0,1:T(8,128)S(1)}, f32[4,3,3,65,129]{4,3,2,0,1:T(8,128)}, u32[]{:S(2)}) copy-start(f32[4,3,3,65,129]{4,3,2,0,1:T(8,128)} %copy-done) | copy-start | bytes 3622324
  108.8 1.7 %copy-start.5 = (f32[2,64,128]{2,1,0:T(8,128)S(1)}, f32[2,64,128]{2,1,0:T(8,128)}, u32[]{:S(2)}) copy-start(f32[2,64,128]{2,1,0:T(8,128)} %param.2) | copy-start | bytes 196612
  108.8 1.7 %copy-start.10 = (f32[2,64,128]{2,1,0:T(8,128)S(1)}, f32[2,64,128]{2,1,0:T(8,128)}, u32[]{:S(2)}) copy-start(f32[2,64,128]{2,1,0:T(8,128)} %copy-done.8) | copy-start | bytes 196612
  108.8 1.7 %copy-start.12 = (f32[2,64,128]{2,1,0:T(8,128)S(1)}, f32[2,64,128]{2,1,0:T(8,128)}, u32[]{:S(2)}) copy-start(f32[2,64,128]{2,1,0:T(8,128)} %copy-done.11) | copy-start | bytes 196612
  112.5 45.9 %all-to-all-start = ((f32[4,2,64,128]{3,1,0,2:T(2,128)}), f32[4,2,64,128]{3,1,0,2:T(2,128)S(1)}, u32[]{:S(2)}, u32[]{:S(2)}) async-start(f32[4,2,64,128]{3,1,0,2:T(2,128)} %copy.8), calls=%async_computation | async-start | bytes 524288 | tf_op jit(solution)/shard_map/all_to_all | solution.py:97
where the time goes:
time: 160 us; the launch traced here: 159 us
  blocking collectives  85.9 us (54%)
  waiting for transfers between devices  30.2 us (19%)
  starting transfers between devices  22 us (14%)
  other arithmetic  12.8 us (8%)
  local copies, waits for them, and re-layouts  7.36 us (5%)
    psum x2, blocking collectives, local(): lax.psum((sizes_local, weighted), ('gx', 'gy', 'gz'))  85.9 us
    ppermute x4, waiting for transfers between devices, with_halo(): lax.ppermute(lax.slice_in_dim(block, block.shape[dim] - width, None, axis...  17.6 us
    ppermute x4, starting transfers between devices, with_halo(): lax.ppermute(lax.slice_in_dim(block, block.shape[dim] - width, None, axis...  12.9 us
    ppermute x4, waiting for transfers between devices, with_halo(): lax.ppermute(lax.slice_in_dim(block, 0, width, axis=dim), axis, backward)  12.6 us
    ppermute x4, starting transfers between devices, with_halo(): lax.ppermute(lax.slice_in_dim(block, 0, width, axis=dim), axis, backward)  5.16 us
    unnamed x36, local copies, waits for them, and re-layouts  4.51 us
    all_to_all x1, starting transfers between devices, local(): lax.all_to_all(labelling, 'gy', split_axis=2, concat_axis=1, tiled=True)  3.9 us
  transfers between devices with their start and end apart: 9, of which 5 were waited for; matrix products, arithmetic and copies ran while one was open for 0% of the time, Pallas kernels for 0%

commit v1 on v0

v1 whole, which is shorter than its diff:
```python
import functools

import jax
import jax.numpy as jnp
from jax import lax
from jax.experimental import pallas as pl
from jax.experimental.pallas import tpu as pltpu
from jax.sharding import PartitionSpec as P

TAU = 0.25
SIGMA = 0.25
LAMBDA = 0.5
PRIOR = 1.0
HALO = 2
ROWS = 8
LANES = 128
MESH = pl.DeviceIdType.MESH


def project_simplex(v):
    a, b, c, d = v
    hi1, lo1 = jnp.maximum(a, b), jnp.minimum(a, b)
    hi2, lo2 = jnp.maximum(c, d), jnp.minimum(c, d)
    s1, s2 = a + b, c + d
    top1 = jnp.maximum(hi1, hi2)
    top2 = jnp.maximum(hi1 + hi2, jnp.maximum(s1, s2))
    top3 = jnp.maximum(s1 + hi2, s2 + hi1)
    top4 = s1 + s2
    t = jnp.maximum(
        jnp.maximum(top1 - 1.0, top2 * 0.5 - 0.5),
        jnp.maximum(top3 * (1.0 / 3.0) - (1.0 / 3.0), top4 * 0.25 - 0.25),
    )
    return [jnp.maximum(x - t, 0.0) for x in v]


def kernel(cfg, levels_ref, vol_ref, lab_ref, cen_ref, vin, buf, rows, volt, s1_ref, l1_ref, p_ref, l2_ref,
           stage, sum_src, sum_plane, sum_line, vin_sem, own_sem, x_send, x_recv, h_send, h_recv,
           z_send, z_recv, a_send, a_recv, out_sem):
    nx, ny, nz, G, X, Z, T = cfg
    how_many = 4
    lx, ly, lz = T * G, ny // G, LANES
    ye = ly + 2 * HALO
    xe = lx + 2 * HALO
    J = volt.shape[0]
    win = buf.shape[1] - 16
    gx, gy, gz = lax.axis_index("gx"), lax.axis_index("gy"), lax.axis_index("gz")
    tiles = lz // ROWS + 2

    load = pltpu.make_async_copy(vol_ref, vin, vin_sem)
    load.start()

    plane = X * G
    me_plane = gx * G + gy
    plane_peers = []
    for d in range(1, plane):
        q = lax.rem(me_plane + d, plane)
        plane_peers.append({"gx": q // G, "gy": lax.rem(q, G), "gz": gz})
    line_peers = [{"gx": gx, "gy": gy, "gz": lax.rem(gz + d, Z)} for d in range(1, Z)]
    barrier = pltpu.get_barrier_semaphore()
    for peer in plane_peers + line_peers:
        pl.semaphore_signal(barrier, inc=1, device_id=peer, device_id_type=MESH)
    pl.semaphore_wait(barrier, len(plane_peers) + len(line_peers))
    load.wait()

    def window(g):
        start = jnp.clip(g * ly - 8, 0, ny - win)
        return pl.multiple_of(start, 8), pl.multiple_of(start - (g * ly - 16), 8)

    sends = []
    for d in range(1, G):
        g = lax.rem(gy + d, G)
        src, dst = window(g)
        c = pltpu.make_async_remote_copy(
            vin.at[:, pl.ds(src, win), :], buf.at[pl.ds(HALO + gy * T, T), pl.ds(dst, win), :],
            x_send.at[d], x_recv.at[gy], device_id={"gx": gx, "gy": g, "gz": gz}, device_id_type=MESH)
        c.start()
        sends.append(c)

    def halo(up, g):
        src, dst = window(g)
        return pltpu.make_async_remote_copy(
            vin.at[pl.ds(T - HALO if up else 0, HALO), pl.ds(src, win), :],
            buf.at[pl.ds(0 if up else HALO + lx, HALO), pl.ds(dst, win), :],
            h_send.at[int(up), g], h_recv.at[int(up)],
            device_id={"gx": gx + 1 if up else gx - 1, "gy": g, "gz": gz}, device_id_type=MESH)

    send_up = (gy == G - 1) & (gx < X - 1)
    send_down = (gy == 0) & (gx > 0)

    @pl.when(send_up)
    def _():
        for g in range(G):
            halo(True, g).start()

    @pl.when(send_down)
    def _():
        for g in range(G):
            halo(False, g).start()

    src, dst = window(gy)
    own = pltpu.make_async_copy(
        vin.at[:, pl.ds(src, win), :], buf.at[pl.ds(HALO + gy * T, T), pl.ds(dst, win), :], own_sem)
    own.start()

    base = [levels_ref[l].astype(jnp.float32) * (1.0 / 255.0) for l in range(how_many)]
    row = lax.broadcasted_iota(jnp.int32, (ROWS, LANES), 0)
    lane = lax.broadcasted_iota(jnp.int32, (ROWS, LANES), 1)
    part, yloc = lane // ye, lane % ye
    x0, y0, z0 = gx * lx - HALO, gy * ly - HALO, gz * lz
    yg = y0 + yloc
    step = TAU * SIGMA
    my = jnp.where((yg >= 0) & (yg < ny - 1), step, 0.0)
    mx, inside, mine = [], [], []
    for j in range(J):
        xloc = part * J + j
        xg = x0 + xloc
        mx.append(jnp.where((xg >= 0) & (xg < nx - 1), step, 0.0))
        inside.append((xg >= 0) & (xg < nx) & (yg >= 0) & (yg < ny) & (xloc < xe))
        mine.append(jnp.where((xloc >= HALO) & (xloc < HALO + lx) & (yloc >= HALO) & (yloc < HALO + ly), 1.0, 0.0))

    def mz(i):
        zg = z0 + (i - 1) * ROWS + row
        return jnp.where((zg >= 0) & (zg < nz - 1), step, 0.0)

    own.wait()
    for d in range(1, G):
        g = lax.rem(gy + d, G)
        pltpu.make_async_remote_copy(
            vin.at[:, pl.ds(src, win), :], buf.at[pl.ds(HALO + g * T, T), pl.ds(dst, win), :],
            x_send.at[d], x_recv.at[g], device_id={"gx": gx, "gy": g, "gz": gz}, device_id_type=MESH).wait_recv()

    def halo_in(up):
        return pltpu.make_async_remote_copy(
            vin.at[pl.ds(0, HALO), pl.ds(src, win), :],
            buf.at[pl.ds(0 if up else HALO + lx, HALO), pl.ds(dst, win), :],
            h_send.at[int(up), 0], h_recv.at[int(up)],
            device_id={"gx": gx, "gy": lax.rem(gy + 1, G), "gz": gz}, device_id_type=MESH)

    @pl.when(gx > 0)
    def _():
        halo_in(True).wait_recv()

    @pl.when(gx < X - 1)
    def _():
        halo_in(False).wait_recv()

    for j in range(J):
        rows[j] = jnp.zeros((LANES, LANES), jnp.float32)
        for i in range(-(-(xe - j) // J)):
            rows[j, i * ye:(i + 1) * ye, :] = buf[i * J + j, 16 - HALO:16 - HALO + ye, :]
    for j in range(J):
        t = rows[j].T
        keep = jnp.broadcast_to(inside[j][:1], (LANES, LANES))
        volt[j, ROWS:ROWS + lz, :] = jnp.where(keep, t, 0.0)

    def z_copy(up):
        return pltpu.make_async_remote_copy(
            volt.at[:, pl.ds(lz if up else ROWS, ROWS), :],
            volt.at[:, pl.ds(0 if up else ROWS + lz, ROWS), :],
            z_send.at[int(up)], z_recv.at[int(up)],
            device_id={"gx": gx, "gy": gy, "gz": gz + 1 if up else gz - 1}, device_id_type=MESH)

    zero = jnp.zeros((J, ROWS, LANES), jnp.float32)

    @pl.when(gz < Z - 1)
    def _():
        z_copy(True).start()

    @pl.when(gz > 0)
    def _():
        z_copy(False).start()

    @pl.when(gz == 0)
    def _():
        volt[:, 0:ROWS, :] = zero

    @pl.when(gz == Z - 1)
    def _():
        volt[:, ROWS + lz:, :] = zero

    @pl.when(gz > 0)
    def _():
        z_copy(True).wait_recv()

    @pl.when(gz < Z - 1)
    def _():
        z_copy(False).wait_recv()

    def at(ref, l, j, i):
        return ref[l, j, pl.ds(pl.multiple_of(i * ROWS, ROWS), ROWS), :]

    def vtile(j, i):
        return volt[j, pl.ds(pl.multiple_of(i * ROWS, ROWS), ROWS), :]

    base_a = [2.0 * TAU * b for b in base]
    base_b = [TAU * b * b for b in base]

    def pull(v):
        return [base_a[l] * v - base_b[l] for l in range(how_many)]

    def start_labels(i):
        return [project_simplex(pull(vtile(j, i))) for j in range(J)]

    def dual_step(s, sn, before, mzi):
        sz = [pltpu.roll(jnp.where(row == 0, sn[j], s[j]), ROWS - 1, 0) for j in range(J)]
        sy = [pltpu.roll(s[j], LANES - 1, 1) for j in range(J)]
        sx = s[1:] + [pltpu.roll(s[0], LANES - ye, 1)]
        px, py, pz = [], [], []
        for j in range(J):
            ax, ay, az = mx[j] * (sx[j] - s[j]), my * (sy[j] - s[j]), mzi * (sz[j] - s[j])
            if before is not None:
                ax, ay, az = ax + before[0][j], ay + before[1][j], az + before[2][j]
            shrink = jnp.minimum(1.0, (TAU * LAMBDA) * lax.rsqrt(ax * ax + ay * ay + az * az))
            px.append(ax * shrink)
            py.append(ay * shrink)
            pz.append(az * shrink)
        return px, py, pz

    def divergence(px, py, pz, pz_before):
        bx = [pltpu.roll(px[J - 1], ye, 1)] + px[:-1]
        out = []
        for j in range(J):
            by = pltpu.roll(py[j], 1, 1)
            bz = pltpu.roll(jnp.where(row == ROWS - 1, pz_before[j], pz[j]), 1, 0)
            out.append(((px[j] - bx[j]) + (py[j] - by)) + (pz[j] - bz))
        return out

    nothing = jnp.zeros((ROWS, LANES), jnp.float32)

    def first(i, carry):
        lab, prev, acc = carry
        ahead = start_labels(jnp.minimum(i + 1, tiles - 1))
        mzi = mz(i)
        here = pl.ds(pl.multiple_of(i * ROWS, ROWS), ROWS)
        own_rows = jnp.where((i > 0) & (i < tiles - 1), 1.0, 0.0)
        u = [[] for j in range(J)]
        new_prev = []
        v = [vtile(j, i) for j in range(J)]
        w = [pull(v[j]) for j in range(J)]
        for l in range(how_many):
            s = [lab[j][l] for j in range(J)]
            px, py, pz = dual_step(s, [ahead[j][l] for j in range(J)], None, mzi)
            div = divergence(px, py, pz, prev[l])
            for j in range(J):
                p_ref[0, l, j, here, :] = px[j]
                p_ref[1, l, j, here, :] = py[j]
                p_ref[2, l, j, here, :] = pz[j]
                u[j].append(s[j] + (div[j] + w[j][l]))
            new_prev.append(pz)
        acc = list(acc)
        for j in range(J):
            new = project_simplex(u[j])
            m = mine[j] * own_rows
            vm = v[j] * m
            for l in range(how_many):
                l1_ref[l, j, here, :] = new[l]
                s1_ref[l, j, here, :] = 2.0 * new[l] - lab[j][l]
                acc[l] = acc[l] + new[l] * m
                acc[how_many + l] = acc[how_many + l] + new[l] * vm
        return ahead, new_prev, acc

    no_prev = [[nothing] * J for l in range(how_many)]
    _, _, acc = lax.fori_loop(0, tiles, first, (start_labels(0), no_prev, [nothing] * (2 * how_many)))

    def reduce_start(k, acc):
        sum_src[k, 0] = jnp.concatenate([jnp.sum(a, axis=0, keepdims=True) for a in acc], axis=0)
        sum_plane[k, me_plane] = sum_src[k, 0]
        out = []
        for d, peer in enumerate(plane_peers, 1):
            c = pltpu.make_async_remote_copy(
                sum_src.at[k, 0], sum_plane.at[k, me_plane], a_send.at[k, d], a_recv.at[k, me_plane],
                device_id=peer, device_id_type=MESH)
            c.start()
            out.append(c)
        return out

    def reduce_finish(k):
        out = []
        for d, peer in enumerate(plane_peers, 1):
            q = lax.rem(me_plane + d, plane)
            pltpu.make_async_remote_copy(
                sum_src.at[k, 0], sum_plane.at[k, q], a_send.at[k, d], a_recv.at[k, q],
                device_id=peer, device_id_type=MESH).wait_recv()
        total = sum_plane[k, 0]
        for q in range(1, plane):
            total = total + sum_plane[k, q]
        sum_src[k, 1] = total
        sum_line[k, gz] = total
        for d, peer in enumerate(line_peers, 1):
            c = pltpu.make_async_remote_copy(
                sum_src.at[k, 1], sum_line.at[k, gz], a_send.at[k, plane + d], a_recv.at[k, plane + gz],
                device_id=peer, device_id_type=MESH)
            c.start()
            out.append(c)
        for d, peer in enumerate(line_peers, 1):
            q = lax.rem(gz + d, Z)
            pltpu.make_async_remote_copy(
                sum_src.at[k, 1], sum_line.at[k, q], a_send.at[k, plane + d], a_recv.at[k, plane + q],
                device_id=peer, device_id_type=MESH).wait_recv()
        total = sum_line[k, 0]
        for q in range(1, Z):
            total = total + sum_line[k, q]
        total = jnp.broadcast_to(jnp.sum(total, axis=1, keepdims=True), (ROWS, LANES))
        centers = []
        for l in range(how_many):
            size, weighted = total[l:l + 1], total[how_many + l:how_many + l + 1]
            centers.append((weighted + PRIOR * base[l]) / (size + PRIOR))
        return centers, out

    sends += reduce_start(0, acc)

    def second(i, prev):
        mzi = mz(i)
        here = pl.ds(pl.multiple_of(i * ROWS, ROWS), ROWS)
        new_prev = []
        for l in range(how_many):
            s = [at(s1_ref, l, j, i) for j in range(J)]
            sn = [at(s1_ref, l, j, i + 1) for j in range(J)]
            before = [[p_ref[k, l, j, here, :] for j in range(J)] for k in range(3)]
            px, py, pz = dual_step(s, sn, before, mzi)
            div = divergence(px, py, pz, prev[l])
            for j in range(J):
                l1_ref[l, j, here, :] = l1_ref[l, j, here, :] + div[j]
            new_prev.append(pz)
        return new_prev

    lax.fori_loop(0, tiles - 1, second, no_prev)

    centers, more = reduce_finish(0)
    sends += more
    cen_a = [jnp.broadcast_to(2.0 * TAU * c, (ROWS, LANES)) for c in centers]
    cen_b = [jnp.broadcast_to(TAU * c * c, (ROWS, LANES)) for c in centers]

    def third(i, acc):
        acc = list(acc)
        there = pl.ds(pl.multiple_of((i - 1) * ROWS, ROWS), ROWS)
        for j in range(J):
            v = vtile(j, i)
            new = project_simplex([at(l1_ref, l, j, i) + (cen_a[l] * v - cen_b[l]) for l in range(how_many)])
            vm = v * mine[j]
            for l in range(how_many):
                l2_ref[l, j, there, :] = new[l]
                acc[l] = acc[l] + new[l] * mine[j]
                acc[how_many + l] = acc[how_many + l] + new[l] * vm
        return acc

    acc = lax.fori_loop(1, tiles - 1, third, [nothing] * (2 * how_many))
    sends += reduce_start(1, acc)

    outs = []
    for l in range(how_many):
        for j in range(J):
            rows[j] = l2_ref[l, j].T
            for i in range(-(-(xe - j) // J)):
                x = i * J + j - HALO
                if 0 <= x < lx:
                    stage[l, x] = rows[j, i * ye + HALO:i * ye + HALO + ly, :]
        c = pltpu.make_async_copy(stage.at[l], lab_ref.at[l], out_sem.at[l])
        c.start()
        outs.append(c)

    centers, more = reduce_finish(1)
    sends += more
    for l in range(how_many):
        cen_ref[l] = centers[l][0, 0]
    for c in outs:
        c.wait()
    for c in sends:
        c.wait_send()

    @pl.when(send_up)
    def _():
        for g in range(G):
            halo(True, g).wait_send()

    @pl.when(send_down)
    def _():
        for g in range(G):
            halo(False, g).wait_send()

    @pl.when(gz < Z - 1)
    def _():
        z_copy(True).wait_send()

    @pl.when(gz > 0)
    def _():
        z_copy(False).wait_send()


def solution(mesh):
    X, G, Z = mesh.shape["gx"], mesh.shape["gy"], mesh.shape["gz"]

    def local(volume, levels):
        T, ny, lz = volume.shape
        nx, nz = T * X * G, lz * Z
        lx, ly = T * G, ny // G
        ye, xe = ly + 2 * HALO, lx + 2 * HALO
        J = -(-xe // (LANES // ye))
        win = min(ny, ly + 16)
        n = levels.shape[0]
        f32 = jnp.float32
        dma = pltpu.SemaphoreType.DMA
        zrows = lz + 2 * ROWS
        return pl.pallas_call(
            functools.partial(kernel, (nx, ny, nz, G, X, Z, T)),
            out_shape=(jax.ShapeDtypeStruct((n, lx, ly, lz), f32), jax.ShapeDtypeStruct((n,), f32)),
            in_specs=[pl.BlockSpec(memory_space=pltpu.SMEM), pl.BlockSpec(memory_space=pl.ANY)],
            out_specs=(pl.BlockSpec(memory_space=pl.ANY), pl.BlockSpec(memory_space=pltpu.SMEM)),
            scratch_shapes=[
                pltpu.VMEM((T, ny, lz), f32),
                pltpu.VMEM((xe, win + 16, lz), f32),
                pltpu.VMEM((J, LANES, LANES), f32),
                pltpu.VMEM((J, zrows, LANES), f32),
                pltpu.VMEM((n, J, zrows, LANES), f32),
                pltpu.VMEM((n, J, zrows, LANES), f32),
                pltpu.VMEM((3, n, J, zrows, LANES), f32),
                pltpu.VMEM((n, J, lz, LANES), f32),
                pltpu.VMEM((n, lx, ly, lz), f32),
                pltpu.VMEM((2, 2, ROWS, LANES), f32),
                pltpu.VMEM((2, X * G, ROWS, LANES), f32),
                pltpu.VMEM((2, Z, ROWS, LANES), f32),
                dma, dma, dma((G,)), dma((G,)), dma((2, G)), dma((2,)), dma((2,)), dma((2,)),
                dma((2, X * G + Z)), dma((2, X * G + Z)), dma((n,)),
            ],
            compiler_params=pltpu.CompilerParams(collective_id=0, has_side_effects=True),
        )(levels, volume)

    return jax.shard_map(
        local,
        mesh=mesh,
        in_specs=(P(("gx", "gy"), None, "gz"), P()),
        out_specs=(P(None, "gx", "gy", "gz"), P()),
        check_vma=False,
    )
```

time: 160 us -> 33.8 us (0.21)
  blocking collectives: 85.9 us -> 0 us
  Pallas kernels: 0 us -> 30.8 us
  waiting for transfers between devices: 30.2 us -> 0 us
  starting transfers between devices: 22 us -> 0 us
  other arithmetic: 12.8 us -> 0 us
  local copies, waits for them, and re-layouts: 7.36 us -> 2.19 us
    psum x2 -> x0, blocking collectives: 85.9 us -> none  [local(): lax.psum((sizes_local, weighted), ('gx', 'gy', 'gz'))]
    pallas_call x0 -> x1, Pallas kernels: none -> 30.8 us  [local(): pl.pallas_call(functools.partial(kernel, (nx, ny, nz, G, X, Z, T)), out_s...]
    ppermute x8 -> x0, waiting for transfers between devices: 30.2 us -> none  [the longest x4 17.6 us: with_halo(): lax.ppermute(lax.slice_in_dim(block, block.shape[dim] - width, None, axis...]
    ppermute x8 -> x0, starting transfers between devices: 18.1 us -> none  [the longest x4 12.9 us: with_halo(): lax.ppermute(lax.slice_in_dim(block, block.shape[dim] - width, None, axis...]
    all_to_all x1 -> x0, starting transfers between devices: 3.9 us -> none  [local(): lax.all_to_all(labelling, 'gy', split_axis=2, concat_axis=1, tiled=True)]
    concatenate x4 -> x0, other arithmetic: 3.19 us -> none  [with_halo(): block = jnp.concatenate([low, block, high], axis=dim)]
    unnamed x36 -> x4, local copies, waits for them, and re-layouts: 4.51 us -> 2.19 us
    mul x5 -> x0, other arithmetic: 2.03 us -> none  [the longest x4 1.8 us: local(): dual_field = stepped * shrink[:, None]]
  transfers between devices with their start and end apart: 9 -> 0, of which waited for: 5 -> 0; matrix products, arithmetic and copies ran while one was open for 0% -> 0% of each run, Pallas kernels for 0% -> 0%
where the time goes in v1:
time: 33.8 us; the launch traced here: 33.7 us
  Pallas kernels  30.8 us (91%)
  local copies, waits for them, and re-layouts  2.19 us (6%)
  between operations  0.65 us (2%)
    pallas_call x1, Pallas kernels, local(): pl.pallas_call(functools.partial(kernel, (nx, ny, nz, G, X, Z, T)), out_s...  30.8 us
    unnamed x4, local copies, waits for them, and re-layouts  2.19 us

profile of v1, /device:TPU:0, one launch (start us, length us, event | category | flops | bytes accessed | tf_op | source)
XLA Modules:
  0.0 33.7 jit_solution(5193024844794751866)
XLA Ops:
  0.6 30.8 %shard_map.41 = (f32[4,8,16,128]{3,2,1,0:T(8,128)}, f32[4]{0:T(128)}) custom-call(s32[4]{0:T(128)} %levels_ref.1, f32[2,64,128]{2,1,0:T(8,128)} %vol_ref.1), custom_call_target="tpu_custom_call" | custom-call | tf_op jit(solution)/shard_map/pallas_call | solution.py:404
  31.5 0.0 copy-start
  31.5 1.7 %copy.6 = f32[4,8,16,128]{3,2,1,0:T(8,128)} copy(f32[4,8,16,128]{3,2,1,0:T(8,128)} %get-tuple-element.4) | data formatting | bytes 524288
  33.1 0.0 copy-done
  33.2 0.5 %copy.7 = f32[4]{0:T(128)} copy(f32[4]{0:T(128)S(1)} %copy-done) | data formatting | bytes 32
Async XLA Ops:
  31.5 1.7 %copy-start = (f32[4]{0:T(128)S(1)}, f32[4]{0:T(128)}, u32[]{:S(2)}) copy-start(f32[4]{0:T(128)} %get-tuple-element.5) | copy-start | bytes 52

commit v2 on v1

--- a/solution.py
+++ b/solution.py
@@ -34,8 +34,8 @@
 
 
 def kernel(cfg, levels_ref, vol_ref, lab_ref, cen_ref, vin, buf, rows, volt, s1_ref, l1_ref, p_ref, l2_ref,
-           stage, sum_src, sum_plane, sum_line, vin_sem, own_sem, x_send, x_recv, h_send, h_recv,
-           z_send, z_recv, a_send, a_recv, out_sem):
+           stage, sum_src, sum_all, vin_sem, own_sem, x_send, x_recv, h_send, h_recv,
+           z_send, z_recv, a_send, a_recv, out_sem, far):
     nx, ny, nz, G, X, Z, T = cfg
     how_many = 4
     lx, ly, lz = T * G, ny // G, LANES
@@ -55,11 +55,22 @@
     for d in range(1, plane):
         q = lax.rem(me_plane + d, plane)
         plane_peers.append({"gx": q // G, "gy": lax.rem(q, G), "gz": gz})
-    line_peers = [{"gx": gx, "gy": gy, "gz": lax.rem(gz + d, Z)} for d in range(1, Z)]
     barrier = pltpu.get_barrier_semaphore()
-    for peer in plane_peers + line_peers:
+    for peer in plane_peers:
         pl.semaphore_signal(barrier, inc=1, device_id=peer, device_id_type=MESH)
-    pl.semaphore_wait(barrier, len(plane_peers) + len(line_peers))
+    above = {"gx": gx, "gy": gy, "gz": gz + 1}
+    below = {"gx": gx, "gy": gy, "gz": gz - 1}
+    has_above, has_below = gz < Z - 1, gz > 0
+
+    @pl.when(has_above)
+    def _():
+        pl.semaphore_signal(barrier, inc=1, device_id=above, device_id_type=MESH)
+
+    @pl.when(has_below)
+    def _():
+        pl.semaphore_signal(barrier, inc=1, device_id=below, device_id_type=MESH)
+
+    pl.semaphore_wait(barrier, plane - 1 + has_above.astype(jnp.int32) + has_below.astype(jnp.int32))
     load.wait()
 
     def window(g):
@@ -96,6 +107,23 @@
     def _():
         for g in range(G):
             halo(False, g).start()
+
+    @pl.when(jnp.logical_not(has_below) & has_above)
+    def _():
+        pl.semaphore_signal(far.at[1], inc=1, device_id=above, device_id_type=MESH)
+
+    @pl.when(has_above)
+    def _():
+        pl.semaphore_wait(far.at[0], 1)
+
+    @pl.when(has_below)
+    def _():
+        pl.semaphore_signal(far.at[0], inc=1, device_id=below, device_id_type=MESH)
+        pl.semaphore_wait(far.at[1], 1)
+
+    @pl.when(has_below & has_above)
+    def _():
+        pl.semaphore_signal(far.at[1], inc=1, device_id=above, device_id_type=MESH)
 
     src, dst = window(gy)
     own = pltpu.make_async_copy(
@@ -177,14 +205,6 @@
     @pl.when(gz == Z - 1)
     def _():
         volt[:, ROWS + lz:, :] = zero
-
-    @pl.when(gz > 0)
-    def _():
-        z_copy(True).wait_recv()
-
-    @pl.when(gz < Z - 1)
-    def _():
-        z_copy(False).wait_recv()
 
     def at(ref, l, j, i):
         return ref[l, j, pl.ds(pl.multiple_of(i * ROWS, ROWS), ROWS), :]
@@ -260,54 +280,58 @@
         return ahead, new_prev, acc
 
     no_prev = [[nothing] * J for l in range(how_many)]
-    _, _, acc = lax.fori_loop(0, tiles, first, (start_labels(0), no_prev, [nothing] * (2 * how_many)))
+    one, two = start_labels(1), start_labels(2)
+    prev = [dual_step([one[j][l] for j in range(J)], [two[j][l] for j in range(J)], None, mz(1))[2]
+            for l in range(how_many)]
+    _, _, acc = carry = lax.fori_loop(2, tiles - 2, first, (two, prev, [nothing] * (2 * how_many)))
+
+    @pl.when(gz > 0)
+    def _():
+        z_copy(True).wait_recv()
+
+    @pl.when(gz < Z - 1)
+    def _():
+        z_copy(False).wait_recv()
+
+    _, _, acc = lax.fori_loop(tiles - 2, tiles, first, (start_labels(tiles - 2), carry[1], acc))
+    _, _, acc = lax.fori_loop(0, 2, first, (start_labels(0), no_prev, acc))
+
+    N = X * G * Z
+    me = me_plane * Z + gz
+    xs = [lax.rem(gx + d, X) for d in range(X)]
+    gs = [lax.rem(gy + d, G) for d in range(G)]
+    zs = [lax.rem(gz + d, Z) for d in range(Z)]
+    offsets = [(a, b, c) for a in range(X) for b in range(G) for c in range(Z)][:0:-1]
 
     def reduce_start(k, acc):
-        sum_src[k, 0] = jnp.concatenate([jnp.sum(a, axis=0, keepdims=True) for a in acc], axis=0)
-        sum_plane[k, me_plane] = sum_src[k, 0]
-        out = []
-        for d, peer in enumerate(plane_peers, 1):
-            c = pltpu.make_async_remote_copy(
-                sum_src.at[k, 0], sum_plane.at[k, me_plane], a_send.at[k, d], a_recv.at[k, me_plane],
-                device_id=peer, device_id_type=MESH)
-            c.start()
-            out.append(c)
-        return out
+        t = jnp.concatenate([jnp.sum(a, axis=0, keepdims=True) for a in acc], axis=0)
+        t = jnp.where(row == lane, jnp.sum(t, axis=1, keepdims=True), 0.0)
+        t = jnp.sum(t, axis=0, keepdims=True)
+        sum_src[k] = t
+        sum_all[k, me] = t
+        for a, b, c in offsets:
+            pltpu.make_async_remote_copy(
+                sum_src.at[k], sum_all.at[k, me], a_send.at[k], a_recv.at[k],
+                device_id={"gx": xs[a], "gy": gs[b], "gz": zs[c]}, device_id_type=MESH).start()
+
+    def every(k):
+        part = sum_all.at[k, pl.ds(0, N - 1)]
+        return pltpu.make_async_remote_copy(
+            part, part, a_send.at[k], a_recv.at[k],
+            device_id={"gx": xs[-1], "gy": gs[-1], "gz": zs[-1]}, device_id_type=MESH)
 
     def reduce_finish(k):
-        out = []
-        for d, peer in enumerate(plane_peers, 1):
-            q = lax.rem(me_plane + d, plane)
-            pltpu.make_async_remote_copy(
-                sum_src.at[k, 0], sum_plane.at[k, q], a_send.at[k, d], a_recv.at[k, q],
-                device_id=peer, device_id_type=MESH).wait_recv()
-        total = sum_plane[k, 0]
-        for q in range(1, plane):
-            total = total + sum_plane[k, q]
-        sum_src[k, 1] = total
-        sum_line[k, gz] = total
-        for d, peer in enumerate(line_peers, 1):
-            c = pltpu.make_async_remote_copy(
-                sum_src.at[k, 1], sum_line.at[k, gz], a_send.at[k, plane + d], a_recv.at[k, plane + gz],
-                device_id=peer, device_id_type=MESH)
-            c.start()
-            out.append(c)
-        for d, peer in enumerate(line_peers, 1):
-            q = lax.rem(gz + d, Z)
-            pltpu.make_async_remote_copy(
-                sum_src.at[k, 1], sum_line.at[k, q], a_send.at[k, plane + d], a_recv.at[k, plane + q],
-                device_id=peer, device_id_type=MESH).wait_recv()
-        total = sum_line[k, 0]
-        for q in range(1, Z):
-            total = total + sum_line[k, q]
-        total = jnp.broadcast_to(jnp.sum(total, axis=1, keepdims=True), (ROWS, LANES))
-        centers = []
+        every(k).wait_recv()
+        terms = [sum_all[k, q] for q in range(N)]
+        while len(terms) > 1:
+            terms = [sum(terms[q:q + 2][1:], terms[q]) for q in range(0, len(terms), 2)]
+        total = terms[0]
+        start = jnp.zeros((1, LANES), jnp.float32)
         for l in range(how_many):
-            size, weighted = total[l:l + 1], total[how_many + l:how_many + l + 1]
-            centers.append((weighted + PRIOR * base[l]) / (size + PRIOR))
-        return centers, out
-
-    sends += reduce_start(0, acc)
+            start = jnp.where(lane[:1] == l, PRIOR * base[l], start)
+        return (pltpu.roll(total, LANES - how_many, 1) + start) / (total + PRIOR)
+
+    reduce_start(0, acc)
 
     def second(i, prev):
         mzi = mz(i)
@@ -326,10 +350,10 @@
 
     lax.fori_loop(0, tiles - 1, second, no_prev)
 
-    centers, more = reduce_finish(0)
-    sends += more
-    cen_a = [jnp.broadcast_to(2.0 * TAU * c, (ROWS, LANES)) for c in centers]
-    cen_b = [jnp.broadcast_to(TAU * c * c, (ROWS, LANES)) for c in centers]
+    centers = reduce_finish(0)
+    centers = [jnp.broadcast_to(centers[:, l:l + 1], (ROWS, LANES)) for l in range(how_many)]
+    cen_a = [2.0 * TAU * c for c in centers]
+    cen_b = [TAU * c * c for c in centers]
 
     def third(i, acc):
         acc = list(acc)
@@ -345,7 +369,7 @@
         return acc
 
     acc = lax.fori_loop(1, tiles - 1, third, [nothing] * (2 * how_many))
-    sends += reduce_start(1, acc)
+    reduce_start(1, acc)
 
     outs = []
     for l in range(how_many):
@@ -359,14 +383,15 @@
         c.start()
         outs.append(c)
 
-    centers, more = reduce_finish(1)
-    sends += more
+    centers = reduce_finish(1)
     for l in range(how_many):
-        cen_ref[l] = centers[l][0, 0]
+        cen_ref[l] = centers[0, l]
     for c in outs:
         c.wait()
     for c in sends:
         c.wait_send()
+    every(0).wait_send()
+    every(1).wait_send()
 
     @pl.when(send_up)
     def _():
@@ -416,11 +441,10 @@
                 pltpu.VMEM((3, n, J, zrows, LANES), f32),
                 pltpu.VMEM((n, J, lz, LANES), f32),
                 pltpu.VMEM((n, lx, ly, lz), f32),
-                pltpu.VMEM((2, 2, ROWS, LANES), f32),
-                pltpu.VMEM((2, X * G, ROWS, LANES), f32),
-                pltpu.VMEM((2, Z, ROWS, LANES), f32),
+                pltpu.VMEM((2, 1, LANES), f32),
+                pltpu.VMEM((2, X * G * Z, 1, LANES), f32),
                 dma, dma, dma((G,)), dma((G,)), dma((2, G)), dma((2,)), dma((2,)), dma((2,)),
-                dma((2, X * G + Z)), dma((2, X * G + Z)), dma((n,)),
+                dma((2,)), dma((2,)), dma((n,)), pltpu.SemaphoreType.REGULAR((2,)),
             ],
             compiler_params=pltpu.CompilerParams(collective_id=0, has_side_effects=True),
         )(levels, volume)

time: 33.8 us -> 26.5 us (0.78)
  Pallas kernels: 30.8 us -> 23.6 us
    pallas_call x1, Pallas kernels: 30.8 us -> 23.6 us  [local(): pl.pallas_call(functools.partial(kernel, (nx, ny, nz, G, X, Z, T)), out_s...]
where the time goes in v2:
time: 26.5 us; the launch traced here: 26.4 us
  Pallas kernels  23.6 us (89%)
  local copies, waits for them, and re-layouts  2.19 us (8%)
  between operations  0.65 us (2%)
    pallas_call x1, Pallas kernels, local(): pl.pallas_call(functools.partial(kernel, (nx, ny, nz, G, X, Z, T)), out_s...  23.6 us
    unnamed x4, local copies, waits for them, and re-layouts  2.19 us

profile of v2, /device:TPU:0, one launch (start us, length us, event | category | flops | bytes accessed | tf_op | source)
XLA Modules:
  0.0 26.4 jit_solution(6244550451078657327)
XLA Ops:
  0.6 23.6 %shard_map.41 = (f32[4,8,16,128]{3,2,1,0:T(8,128)}, f32[4]{0:T(128)}) custom-call(s32[4]{0:T(128)} %levels_ref.1, f32[2,64,128]{2,1,0:T(8,128)} %vol_ref.1), custom_call_target="tpu_custom_call" | custom-call | tf_op jit(solution)/shard_map/pallas_call | solution.py:429
  24.2 0.0 copy-start
  24.2 1.7 %copy.6 = f32[4,8,16,128]{3,2,1,0:T(8,128)} copy(f32[4,8,16,128]{3,2,1,0:T(8,128)} %get-tuple-element.4) | data formatting | bytes 524288
  25.9 0.0 copy-done
  25.9 0.5 %copy.7 = f32[4]{0:T(128)} copy(f32[4]{0:T(128)S(1)} %copy-done) | data formatting | bytes 32
Async XLA Ops:
  24.2 1.7 %copy-start = (f32[4]{0:T(128)S(1)}, f32[4]{0:T(128)}, u32[]{:S(2)}) copy-start(f32[4]{0:T(128)} %get-tuple-element.5) | copy-start | bytes 52

commit v3 on v2

--- a/solution.py
+++ b/solution.py
@@ -33,9 +33,9 @@
     return [jnp.maximum(x - t, 0.0) for x in v]
 
 
-def kernel(cfg, levels_ref, vol_ref, lab_ref, cen_ref, vin, buf, rows, volt, s1_ref, l1_ref, p_ref, l2_ref,
-           stage, sum_src, sum_all, vin_sem, own_sem, x_send, x_recv, h_send, h_recv,
-           z_send, z_recv, a_send, a_recv, out_sem, far):
+def kernel(cfg, levels_hbm, vol_ref, lab_ref, cen_ref, vin, buf, rows, volt, s1_ref, l1_ref, p_ref, l2_ref,
+           levels, sum_src, sum_all, vin_sem, own_sem, x_send, x_recv, h_send, h_recv,
+           z_send, z_recv, a_send, a_recv, lev_sem, far):
     nx, ny, nz, G, X, Z, T = cfg
     how_many = 4
     lx, ly, lz = T * G, ny // G, LANES
@@ -48,6 +48,8 @@
 
     load = pltpu.make_async_copy(vol_ref, vin, vin_sem)
     load.start()
+    load_levels = pltpu.make_async_copy(levels_hbm, levels, lev_sem)
+    load_levels.start()
 
     plane = X * G
     me_plane = gx * G + gy
@@ -130,7 +132,8 @@
         vin.at[:, pl.ds(src, win), :], buf.at[pl.ds(HALO + gy * T, T), pl.ds(dst, win), :], own_sem)
     own.start()
 
-    base = [levels_ref[l].astype(jnp.float32) * (1.0 / 255.0) for l in range(how_many)]
+    load_levels.wait()
+    base = [levels[l].astype(jnp.float32) * (1.0 / 255.0) for l in range(how_many)]
     row = lax.broadcasted_iota(jnp.int32, (ROWS, LANES), 0)
     lane = lax.broadcasted_iota(jnp.int32, (ROWS, LANES), 1)
     part, yloc = lane // ye, lane % ye
@@ -371,23 +374,16 @@
     acc = lax.fori_loop(1, tiles - 1, third, [nothing] * (2 * how_many))
     reduce_start(1, acc)
 
-    outs = []
     for l in range(how_many):
         for j in range(J):
             rows[j] = l2_ref[l, j].T
             for i in range(-(-(xe - j) // J)):
                 x = i * J + j - HALO
                 if 0 <= x < lx:
-                    stage[l, x] = rows[j, i * ye + HALO:i * ye + HALO + ly, :]
-        c = pltpu.make_async_copy(stage.at[l], lab_ref.at[l], out_sem.at[l])
-        c.start()
-        outs.append(c)
+                    lab_ref[l, x] = rows[j, i * ye + HALO:i * ye + HALO + ly, :]
 
     centers = reduce_finish(1)
-    for l in range(how_many):
-        cen_ref[l] = centers[0, l]
-    for c in outs:
-        c.wait()
+    cen_ref[...] = centers[0, :how_many]
     for c in sends:
         c.wait_send()
     every(0).wait_send()
@@ -429,8 +425,8 @@
         return pl.pallas_call(
             functools.partial(kernel, (nx, ny, nz, G, X, Z, T)),
             out_shape=(jax.ShapeDtypeStruct((n, lx, ly, lz), f32), jax.ShapeDtypeStruct((n,), f32)),
-            in_specs=[pl.BlockSpec(memory_space=pltpu.SMEM), pl.BlockSpec(memory_space=pl.ANY)],
-            out_specs=(pl.BlockSpec(memory_space=pl.ANY), pl.BlockSpec(memory_space=pltpu.SMEM)),
+            in_specs=[pl.BlockSpec(memory_space=pl.ANY), pl.BlockSpec(memory_space=pl.ANY)],
+            out_specs=(pl.BlockSpec(memory_space=pltpu.VMEM), pl.BlockSpec(memory_space=pltpu.VMEM)),
             scratch_shapes=[
                 pltpu.VMEM((T, ny, lz), f32),
                 pltpu.VMEM((xe, win + 16, lz), f32),
@@ -440,14 +436,14 @@
                 pltpu.VMEM((n, J, zrows, LANES), f32),
                 pltpu.VMEM((3, n, J, zrows, LANES), f32),
                 pltpu.VMEM((n, J, lz, LANES), f32),
-                pltpu.VMEM((n, lx, ly, lz), f32),
+                pltpu.SMEM((n,), jnp.int32),
                 pltpu.VMEM((2, 1, LANES), f32),
                 pltpu.VMEM((2, X * G * Z, 1, LANES), f32),
                 dma, dma, dma((G,)), dma((G,)), dma((2, G)), dma((2,)), dma((2,)), dma((2,)),
-                dma((2,)), dma((2,)), dma((n,)), pltpu.SemaphoreType.REGULAR((2,)),
+                dma((2,)), dma((2,)), dma, pltpu.SemaphoreType.REGULAR((2,)),
             ],
-            compiler_params=pltpu.CompilerParams(collective_id=0, has_side_effects=True),
-        )(levels, volume)
+            compiler_params=pltpu.CompilerParams(collective_id=0, vmem_limit_bytes=16 << 20, has_side_effects=True),
+        )(pltpu.with_memory_space_constraint(levels, pltpu.HBM), pltpu.with_memory_space_constraint(volume, pltpu.HBM))
 
     return jax.shard_map(
         local,

time: 26.5 us -> 24.2 us (0.913)
  Pallas kernels: 23.6 us -> 22.3 us
  local copies, waits for them, and re-layouts: 2.19 us -> 1.22 us
    pallas_call x1, Pallas kernels: 23.6 us -> 22.3 us  [local(): pl.pallas_call(functools.partial(kernel, (nx, ny, nz, G, X, Z, T)), out_s...]
    unnamed x4 -> x2, local copies, waits for them, and re-layouts: 2.19 us -> 1.22 us
where the time goes in v3:
time: 24.2 us; the launch traced here: 24.1 us
  Pallas kernels  22.3 us (92%)
  local copies, waits for them, and re-layouts  1.22 us (5%)
  between operations  0.64 us (3%)
    pallas_call x1, Pallas kernels, local(): pl.pallas_call(functools.partial(kernel, (nx, ny, nz, G, X, Z, T)), out_s...  22.3 us
    unnamed x2, local copies, waits for them, and re-layouts  1.22 us

profile of v3, /device:TPU:0, one launch (start us, length us, event | category | flops | bytes accessed | tf_op | source)
XLA Modules:
  0.0 24.1 jit_solution(13859279389495012914)
XLA Ops:
  0.6 22.3 %shard_map.41 = (f32[4,8,16,128]{3,2,1,0:T(8,128)S(1)}, f32[4]{0:T(128)S(1)}) custom-call(s32[4]{0:T(128)} %levels_hbm.1, f32[2,64,128]{2,1,0:T(8,128)} %vol_ref.1), custom_call_target="tpu_custom_call" | custom-call | tf_op jit(solution)/shard_map/pallas_call | solution.py:425
  22.9 0.7 %copy.6 = f32[4,8,16,128]{3,2,1,0:T(8,128)} copy(f32[4,8,16,128]{3,2,1,0:T(8,128)S(1)} %get-tuple-element.4) | data formatting | bytes 524288
  23.6 0.5 %copy.7 = f32[4]{0:T(128)} copy(f32[4]{0:T(128)S(1)} %get-tuple-element.5) | data formatting | bytes 32

commit v4 on v3

--- a/solution.py
+++ b/solution.py
@@ -42,7 +42,7 @@
     ye = ly + 2 * HALO
     xe = lx + 2 * HALO
     J = volt.shape[0]
-    win = buf.shape[1] - 16
+    win = ye
     gx, gy, gz = lax.axis_index("gx"), lax.axis_index("gy"), lax.axis_index("gz")
     tiles = lz // ROWS + 2
 
@@ -76,15 +76,15 @@
     load.wait()
 
     def window(g):
-        start = jnp.clip(g * ly - 8, 0, ny - win)
-        return pl.multiple_of(start, 8), pl.multiple_of(start - (g * ly - 16), 8)
+        start = jnp.clip(g * ly - HALO, 0, ny - win)
+        return start, start - (g * ly - 2 * HALO)
 
     sends = []
     for d in range(1, G):
         g = lax.rem(gy + d, G)
         src, dst = window(g)
         c = pltpu.make_async_remote_copy(
-            vin.at[:, pl.ds(src, win), :], buf.at[pl.ds(HALO + gy * T, T), pl.ds(dst, win), :],
+            vin.at[:, pl.ds(src, win)], buf.at[pl.ds(HALO + gy * T, T), pl.ds(dst, win)],
             x_send.at[d], x_recv.at[gy], device_id={"gx": gx, "gy": g, "gz": gz}, device_id_type=MESH)
         c.start()
         sends.append(c)
@@ -92,8 +92,8 @@
     def halo(up, g):
         src, dst = window(g)
         return pltpu.make_async_remote_copy(
-            vin.at[pl.ds(T - HALO if up else 0, HALO), pl.ds(src, win), :],
-            buf.at[pl.ds(0 if up else HALO + lx, HALO), pl.ds(dst, win), :],
+            vin.at[pl.ds(T - HALO if up else 0, HALO), pl.ds(src, win)],
+            buf.at[pl.ds(0 if up else HALO + lx, HALO), pl.ds(dst, win)],
             h_send.at[int(up), g], h_recv.at[int(up)],
             device_id={"gx": gx + 1 if up else gx - 1, "gy": g, "gz": gz}, device_id_type=MESH)
 
@@ -110,26 +110,30 @@
         for g in range(G):
             halo(False, g).start()
 
-    @pl.when(jnp.logical_not(has_below) & has_above)
+    upper = gz >= Z // 2
+
+    @pl.when(has_below & jnp.logical_not(has_above))
+    def _():
+        pl.semaphore_signal(far.at[0], inc=1, device_id=below, device_id_type=MESH)
+
+    @pl.when(has_above & jnp.logical_not(has_below))
     def _():
         pl.semaphore_signal(far.at[1], inc=1, device_id=above, device_id_type=MESH)
 
-    @pl.when(has_above)
-    def _():
-        pl.semaphore_wait(far.at[0], 1)
-
-    @pl.when(has_below)
-    def _():
-        pl.semaphore_signal(far.at[0], inc=1, device_id=below, device_id_type=MESH)
-        pl.semaphore_wait(far.at[1], 1)
-
-    @pl.when(has_below & has_above)
-    def _():
-        pl.semaphore_signal(far.at[1], inc=1, device_id=above, device_id_type=MESH)
+    def pass_on(down, up):
+        @pl.when(down)
+        def _():
+            pl.semaphore_wait(far.at[0], 1)
+            pl.semaphore_signal(far.at[0], inc=1, device_id=below, device_id_type=MESH)
+
+        @pl.when(up)
+        def _():
+            pl.semaphore_wait(far.at[1], 1)
+            pl.semaphore_signal(far.at[1], inc=1, device_id=above, device_id_type=MESH)
 
     src, dst = window(gy)
     own = pltpu.make_async_copy(
-        vin.at[:, pl.ds(src, win), :], buf.at[pl.ds(HALO + gy * T, T), pl.ds(dst, win), :], own_sem)
+        vin.at[:, pl.ds(src, win)], buf.at[pl.ds(HALO + gy * T, T), pl.ds(dst, win)], own_sem)
     own.start()
 
     load_levels.wait()
@@ -157,13 +161,13 @@
     for d in range(1, G):
         g = lax.rem(gy + d, G)
         pltpu.make_async_remote_copy(
-            vin.at[:, pl.ds(src, win), :], buf.at[pl.ds(HALO + g * T, T), pl.ds(dst, win), :],
+            vin.at[:, pl.ds(src, win)], buf.at[pl.ds(HALO + g * T, T), pl.ds(dst, win)],
             x_send.at[d], x_recv.at[g], device_id={"gx": gx, "gy": g, "gz": gz}, device_id_type=MESH).wait_recv()
 
     def halo_in(up):
         return pltpu.make_async_remote_copy(
-            vin.at[pl.ds(0, HALO), pl.ds(src, win), :],
-            buf.at[pl.ds(0 if up else HALO + lx, HALO), pl.ds(dst, win), :],
+            vin.at[pl.ds(0, HALO), pl.ds(src, win)],
+            buf.at[pl.ds(0 if up else HALO + lx, HALO), pl.ds(dst, win)],
             h_send.at[int(up), 0], h_recv.at[int(up)],
             device_id={"gx": gx, "gy": lax.rem(gy + 1, G), "gz": gz}, device_id_type=MESH)
 
@@ -174,11 +178,14 @@
     @pl.when(gx < X - 1)
     def _():
         halo_in(False).wait_recv()
+
+    inner = has_above & has_below
+    pass_on(upper & inner, jnp.logical_not(upper) & inner)
 
     for j in range(J):
         rows[j] = jnp.zeros((LANES, LANES), jnp.float32)
         for i in range(-(-(xe - j) // J)):
-            rows[j, i * ye:(i + 1) * ye, :] = buf[i * J + j, 16 - HALO:16 - HALO + ye, :]
+            rows[j, i * ye:(i + 1) * ye, :] = buf[i * J + j, HALO:HALO + ye].reshape(ye, LANES)
     for j in range(J):
         t = rows[j].T
         keep = jnp.broadcast_to(inside[j][:1], (LANES, LANES))
@@ -286,7 +293,10 @@
     one, two = start_labels(1), start_labels(2)
     prev = [dual_step([one[j][l] for j in range(J)], [two[j][l] for j in range(J)], None, mz(1))[2]
             for l in range(how_many)]
-    _, _, acc = carry = lax.fori_loop(2, tiles - 2, first, (two, prev, [nothing] * (2 * how_many)))
+    middle = tiles // 2
+    carry = lax.fori_loop(2, middle, first, (two, prev, [nothing] * (2 * how_many)))
+    pass_on(jnp.logical_not(upper) & inner, upper & inner)
+    carry = lax.fori_loop(middle, tiles - 2, first, carry)
 
     @pl.when(gz > 0)
     def _():
@@ -296,7 +306,7 @@
     def _():
         z_copy(False).wait_recv()
 
-    _, _, acc = lax.fori_loop(tiles - 2, tiles, first, (start_labels(tiles - 2), carry[1], acc))
+    _, _, acc = lax.fori_loop(tiles - 2, tiles, first, carry)
     _, _, acc = lax.fori_loop(0, 2, first, (start_labels(0), no_prev, acc))
 
     N = X * G * Z
@@ -333,6 +343,14 @@
         for l in range(how_many):
             start = jnp.where(lane[:1] == l, PRIOR * base[l], start)
         return (pltpu.roll(total, LANES - how_many, 1) + start) / (total + PRIOR)
+
+    @pl.when(has_above & jnp.logical_not(has_below))
+    def _():
+        pl.semaphore_wait(far.at[0], 1)
+
+    @pl.when(has_below & jnp.logical_not(has_above))
+    def _():
+        pl.semaphore_wait(far.at[1], 1)
 
     reduce_start(0, acc)
 
@@ -417,7 +435,6 @@
         lx, ly = T * G, ny // G
         ye, xe = ly + 2 * HALO, lx + 2 * HALO
         J = -(-xe // (LANES // ye))
-        win = min(ny, ly + 16)
         n = levels.shape[0]
         f32 = jnp.float32
         dma = pltpu.SemaphoreType.DMA
@@ -428,8 +445,8 @@
             in_specs=[pl.BlockSpec(memory_space=pl.ANY), pl.BlockSpec(memory_space=pl.ANY)],
             out_specs=(pl.BlockSpec(memory_space=pltpu.VMEM), pl.BlockSpec(memory_space=pltpu.VMEM)),
             scratch_shapes=[
-                pltpu.VMEM((T, ny, lz), f32),
-                pltpu.VMEM((xe, win + 16, lz), f32),
+                pltpu.VMEM((T, ny, 1, lz), f32),
+                pltpu.VMEM((xe, ye + 2 * HALO, 1, lz), f32),
                 pltpu.VMEM((J, LANES, LANES), f32),
                 pltpu.VMEM((J, zrows, LANES), f32),
                 pltpu.VMEM((n, J, zrows, LANES), f32),
@@ -443,7 +460,8 @@
                 dma((2,)), dma((2,)), dma, pltpu.SemaphoreType.REGULAR((2,)),
             ],
             compiler_params=pltpu.CompilerParams(collective_id=0, vmem_limit_bytes=16 << 20, has_side_effects=True),
-        )(pltpu.with_memory_space_constraint(levels, pltpu.HBM), pltpu.with_memory_space_constraint(volume, pltpu.HBM))
+        )(pltpu.with_memory_space_constraint(levels, pltpu.HBM),
+          pltpu.with_memory_space_constraint(volume.reshape(T, ny, 1, lz), pltpu.HBM))
 
     return jax.shard_map(
         local,

time: 24.2 us -> 23 us (0.950)
  Pallas kernels: 22.3 us -> 21 us
    pallas_call x1, Pallas kernels: 22.3 us -> 21 us  [local(): pl.pallas_call(functools.partial(kernel, (nx, ny, nz, G, X, Z, T)), out_s...]
where the time goes in v4:
time: 23 us; the launch traced here: 22.9 us
  Pallas kernels  21 us (91%)
  local copies, waits for them, and re-layouts  1.22 us (5%)
  between operations  0.64 us (3%)
    pallas_call x1, Pallas kernels, local(): pl.pallas_call(functools.partial(kernel, (nx, ny, nz, G, X, Z, T)), out_s...  21 us
    unnamed x2, local copies, waits for them, and re-layouts  1.22 us

profile of v4, /device:TPU:0, one launch (start us, length us, event | category | flops | bytes accessed | tf_op | source)
XLA Modules:
  0.0 22.9 jit_solution(10069469701710787840)
XLA Ops:
  0.6 21.0 %shard_map.41 = (f32[4,8,16,128]{3,2,1,0:T(8,128)S(1)}, f32[4]{0:T(128)S(1)}) custom-call(s32[4]{0:T(128)} %levels_hbm.1, f32[2,64,1,128]{3,2,1,0:T(1,128)} %bitcast.1), custom_call_target="tpu_custom_call" | custom-call | tf_op jit(solution)/shard_map/pallas_call | solution.py:442
  21.7 0.7 %copy.6 = f32[4,8,16,128]{3,2,1,0:T(8,128)} copy(f32[4,8,16,128]{3,2,1,0:T(8,128)S(1)} %get-tuple-element.4) | data formatting | bytes 524288
  22.4 0.5 %copy.7 = f32[4]{0:T(128)} copy(f32[4]{0:T(128)S(1)} %get-tuple-element.5) | data formatting | bytes 32

commit v5 on v4

--- a/solution.py
+++ b/solution.py
@@ -48,6 +48,16 @@
 
     load = pltpu.make_async_copy(vol_ref, vin, vin_sem)
     load.start()
+    win = ye
+
+    def window(g):
+        start = jnp.clip(g * ly - HALO, 0, ny - win)
+        return start, start - (g * ly - 2 * HALO)
+
+    src, dst = window(gy)
+    own = pltpu.make_async_copy(
+        vol_ref.at[:, pl.ds(src, win)], buf.at[pl.ds(HALO + gy * T, T), pl.ds(dst, win)], own_sem)
+    own.start()
     load_levels = pltpu.make_async_copy(levels_hbm, levels, lev_sem)
     load_levels.start()
 
@@ -75,9 +85,26 @@
     pl.semaphore_wait(barrier, plane - 1 + has_above.astype(jnp.int32) + has_below.astype(jnp.int32))
     load.wait()
 
-    def window(g):
-        start = jnp.clip(g * ly - HALO, 0, ny - win)
-        return start, start - (g * ly - 2 * HALO)
+    def halo(up, g):
+        src, dst = window(g)
+        return pltpu.make_async_remote_copy(
+            vin.at[pl.ds(T - HALO if up else 0, HALO), pl.ds(src, win)],
+            buf.at[pl.ds(0 if up else HALO + lx, HALO), pl.ds(dst, win)],
+            h_send.at[int(up), g], h_recv.at[int(up)],
+            device_id={"gx": gx + 1 if up else gx - 1, "gy": g, "gz": gz}, device_id_type=MESH)
+
+    send_up = (gy == G - 1) & (gx < X - 1)
+    send_down = (gy == 0) & (gx > 0)
+
+    @pl.when(send_up)
+    def _():
+        for g in range(G):
+            halo(True, g).start()
+
+    @pl.when(send_down)
+    def _():
+        for g in range(G):
+            halo(False, g).start()
 
     sends = []
     for d in range(1, G):
@@ -89,27 +116,6 @@
         c.start()
         sends.append(c)
 
-    def halo(up, g):
-        src, dst = window(g)
-        return pltpu.make_async_remote_copy(
-            vin.at[pl.ds(T - HALO if up else 0, HALO), pl.ds(src, win)],
-            buf.at[pl.ds(0 if up else HALO + lx, HALO), pl.ds(dst, win)],
-            h_send.at[int(up), g], h_recv.at[int(up)],
-            device_id={"gx": gx + 1 if up else gx - 1, "gy": g, "gz": gz}, device_id_type=MESH)
-
-    send_up = (gy == G - 1) & (gx < X - 1)
-    send_down = (gy == 0) & (gx > 0)
-
-    @pl.when(send_up)
-    def _():
-        for g in range(G):
-            halo(True, g).start()
-
-    @pl.when(send_down)
-    def _():
-        for g in range(G):
-            halo(False, g).start()
-
     upper = gz >= Z // 2
 
     @pl.when(has_below & jnp.logical_not(has_above))
@@ -131,10 +137,6 @@
             pl.semaphore_wait(far.at[1], 1)
             pl.semaphore_signal(far.at[1], inc=1, device_id=above, device_id_type=MESH)
 
-    src, dst = window(gy)
-    own = pltpu.make_async_copy(
-        vin.at[:, pl.ds(src, win)], buf.at[pl.ds(HALO + gy * T, T), pl.ds(dst, win)], own_sem)
-    own.start()
 
     load_levels.wait()
     base = [levels[l].astype(jnp.float32) * (1.0 / 255.0) for l in range(how_many)]

time: 23 us -> 22.7 us (0.987)
  Pallas kernels: 21 us -> 20.7 us
    pallas_call x1, Pallas kernels: 21 us -> 20.7 us  [local(): pl.pallas_call(functools.partial(kernel, (nx, ny, nz, G, X, Z, T)), out_s...]
where the time goes in v5:
time: 22.7 us; the launch traced here: 22.6 us
  Pallas kernels  20.7 us (91%)
  local copies, waits for them, and re-layouts  1.22 us (5%)
  between operations  0.64 us (3%)
    pallas_call x1, Pallas kernels, local(): pl.pallas_call(functools.partial(kernel, (nx, ny, nz, G, X, Z, T)), out_s...  20.7 us
    unnamed x2, local copies, waits for them, and re-layouts  1.22 us

profile of v5, /device:TPU:0, one launch (start us, length us, event | category | flops | bytes accessed | tf_op | source)
XLA Modules:
  0.0 22.6 jit_solution(3109742409069246738)
XLA Ops:
  0.6 20.7 %shard_map.41 = (f32[4,8,16,128]{3,2,1,0:T(8,128)S(1)}, f32[4]{0:T(128)S(1)}) custom-call(s32[4]{0:T(128)} %levels_hbm.1, f32[2,64,1,128]{3,2,1,0:T(1,128)} %bitcast.1), custom_call_target="tpu_custom_call" | custom-call | tf_op jit(solution)/shard_map/pallas_call | solution.py:444
  21.4 0.7 %copy.6 = f32[4,8,16,128]{3,2,1,0:T(8,128)} copy(f32[4,8,16,128]{3,2,1,0:T(8,128)S(1)} %get-tuple-element.4) | data formatting | bytes 524288
  22.1 0.5 %copy.7 = f32[4]{0:T(128)} copy(f32[4]{0:T(128)S(1)} %get-tuple-element.5) | data formatting | bytes 32
